TPU v7x, 32 devices: a whole 2x2x4 slice. The times are simulated.
32 devices in a mesh: ctx: 8 (over z, core), tp: 4 (over y, x).
Axes of the slice: x: 2, y: 2, z: 4, core: 2. Of those that a mesh axis runs over, the one named last changes fastest.
Arguments:
- tokens: bfloat16 [2, 4096, 8192], P(None, 'ctx', 'tp'), may hold values from -14 to 14
- norm_gain: float32 [8192], replicated, may hold values from 0.5 to 1.5
- span_order: int32 [2, 16], replicated, may hold values from 0 to 15, each once within a row
- w_query: bfloat16 [8192, 4096], P('ctx', 'tp'), may hold values from -0.10122281 to 0.10122281
- w_key: bfloat16 [8192, 1024], P('ctx', 'tp'), may hold values from -0.10122281 to 0.10122281
- value_weight: bfloat16 [8192, 1024], P('ctx', 'tp'), may hold values from -0.0625 to 0.0625
- w_out: bfloat16 [4096, 8192], P('tp', 'ctx'), may hold values from -0.75 to 0.75
Outputs:
- mixed: bfloat16 [2, 4096, 8192], P(None, 'ctx', 'tp')
Inputs may be any that keep to these rules, and one draw needn't show every extreme that they name: Each row of span_order names every one of the 2 * 8 blocks of positions once; stored block b of a sequence holds positions span_order[b] * 256 onwards, in order.
All inputs are finite; a program needn't handle non-finite values.
Results may differ from a plain program's by a relative error of at most 0.014.
Values may be sent and summed in bfloat16 or wider, within the bound.
A program may use at most 128 MiB of HBM per device.

v0:
```python
import math
import jax
import jax.numpy as jnp
from jax import lax
from jax.sharding import PartitionSpec as P

HEAD_DIM = 128
theta_base = 500000.0
norm_eps = 1e-05
masked_score = -1e30


def normalize(flat_rows, norm_gain):
    wide = flat_rows.astype(jnp.float32)
    factor = lax.rsqrt(jnp.mean(wide * wide, axis=-1, keepdims=True) + norm_eps)
    return (wide * factor * norm_gain).astype(jnp.bfloat16)


def positions_of(span_order, first, count, block_rows):
    stored = first + jnp.arange(count, dtype=jnp.int32)
    which = stored // block_rows
    slots = jnp.arange(span_order.shape[1], dtype=jnp.int32)
    picked = jnp.sum(
        jnp.where(slots[None, None, :] == which[None, :, None], span_order[:, None, :], 0), axis=2
    )
    return picked * block_rows + stored % block_rows


def apply_rotation(value_rows, token_position, head_size):
    half = head_size // 2
    freqs = jnp.exp(-(2.0 * jnp.arange(half, dtype=jnp.float32) / head_size) * math.log(theta_base))
    angle = token_position.astype(jnp.float32)[..., None] * freqs
    cosine = jnp.cos(angle)[:, :, None, :]
    sine = jnp.sin(angle)[:, :, None, :]
    front = value_rows[..., :half]
    back = value_rows[..., half:]
    return jnp.concatenate([front * cosine - back * sine, back * cosine + front * sine], axis=-1)


def per_device(tokens, norm_gain, span_order, w_query, w_key, value_weight, w_out):
    sequence_batch, rows_dev, _ = tokens.shape
    head_size = HEAD_DIM
    query_heads = w_query.shape[1] // head_size
    key_heads = w_key.shape[1] // head_size
    group_width = query_heads // key_heads
    block_rows = rows_dev // 2
    total_rows = sequence_batch * rows_dev
    factor = 1.0 / math.sqrt(head_size)
    rank = lax.axis_index("ctx")
    whole = lax.all_gather(tokens, "tp", axis=2, tiled=True)
    normed = normalize(whole.reshape(total_rows, whole.shape[2]), norm_gain)
    query_pos = positions_of(span_order, rank * rows_dev, rows_dev, block_rows)
    latest = jnp.max(query_pos, axis=1)
    stat_shape = (sequence_batch, key_heads, group_width, rows_dev)
    initial = (
        jnp.full(stat_shape, masked_score, jnp.float32),
        jnp.zeros(stat_shape, jnp.float32),
        jnp.zeros(stat_shape + (head_size,), jnp.float32),
    )
    pieces = (
        lax.all_gather(w_query, "ctx", axis=0, tiled=True),
        lax.all_gather(w_key, "ctx", axis=0, tiled=True),
        lax.all_gather(value_weight, "ctx", axis=0, tiled=True),
    )
    query_flat, flattened_key, flattened_value = tuple(
        (jnp.dot(normed, piece, preferred_element_type=jnp.float32) for piece in pieces)
    )
    turned = apply_rotation(
        query_flat.reshape(sequence_batch, rows_dev, query_heads, head_size), query_pos, head_size
    ).astype(jnp.bfloat16)
    query = turned.reshape(sequence_batch, rows_dev, key_heads, group_width, head_size).transpose(
        0, 2, 3, 1, 4
    )
    turned = apply_rotation(
        flattened_key.reshape(sequence_batch, rows_dev, key_heads, head_size), query_pos, head_size
    ).astype(jnp.bfloat16)
    own_values = flattened_value.reshape(sequence_batch, rows_dev, key_heads, head_size).astype(
        jnp.bfloat16
    )
    key_piece = lax.all_gather(turned, "ctx", axis=1, tiled=True)
    value_piece = lax.all_gather(own_values, "ctx", axis=1, tiled=True)
    count = key_piece.shape[1]
    step_rows = 512

    def one_block(index, state):
        first = index * step_rows
        key_block = lax.dynamic_slice_in_dim(key_piece, first, step_rows, 1)
        value_block = lax.dynamic_slice_in_dim(value_piece, first, step_rows, 1)
        key_pos = positions_of(span_order, first, step_rows, block_rows)

        def update(current):
            peak, total, summed = current
            scores = (
                jnp.einsum(
                    "shgqd,skhd->shgqk", query, key_block, preferred_element_type=jnp.float32
                )
                * factor
            )
            allowed = key_pos[:, None, None, None, :] <= query_pos[:, None, None, :, None]
            scores = jnp.where(allowed, scores, masked_score)
            new_peak = jnp.maximum(peak, jnp.max(scores, axis=-1))
            weights = jnp.where(allowed, jnp.exp(scores - new_peak[..., None]), 0.0)
            shrink = jnp.exp(peak - new_peak)
            total = total * shrink + jnp.sum(weights, axis=-1)
            summed = summed * shrink[..., None] + jnp.einsum(
                "shgqk,skhd->shgqd",
                weights.astype(jnp.bfloat16),
                value_block,
                preferred_element_type=jnp.float32,
            )
            return (new_peak, total, summed)

        return lax.cond(
            jnp.all(jnp.min(key_pos, axis=1) > latest), lambda kept: kept, update, state
        )

    peak, total, summed = lax.fori_loop(0, count // step_rows, one_block, initial)
    attended = (summed / total[..., None]).astype(jnp.bfloat16)
    attended = attended.transpose(0, 3, 1, 2, 4).reshape(total_rows, query_heads * head_size)
    terms = jnp.dot(
        attended,
        lax.all_gather(w_out, "ctx", axis=1, tiled=True),
        preferred_element_type=jnp.float32,
    )
    mixed = lax.psum_scatter(terms.astype(jnp.bfloat16), "tp", scatter_dimension=1, tiled=True)
    return mixed.reshape(sequence_batch, rows_dev, mixed.shape[1])


def solution(mesh):
    placed = (
        P(None, "ctx", "tp"),
        P(),
        P(),
        P("ctx", "tp"),
        P("ctx", "tp"),
        P("ctx", "tp"),
        P("tp", "ctx"),
    )
    return jax.shard_map(
        per_device, mesh=mesh, in_specs=placed, out_specs=P(None, "ctx", "tp"), check_vma=False
    )
```

profile of v0, /device:TPU:0, one launch (start us, length us, event | category | flops | bytes accessed | tf_op | source)
XLA Modules:
  0.0 862.1 jit_solution(7252307660646929625)
XLA Ops:
  6.5 0.7 all-gather.10.cloned.1.call-update
  9.5 1.0 multiply_cosine_fusion
  10.5 48.0 %all-gather.10.cloned.1.call-done = bf16[8192,256]{1,0:T(8,128)(2,1)} async-done(((bf16[1024,256]{1,0:T(8,128)(2,1)}), bf16[8192,256]{1,0:T(8,128)(2,1)}) %all-gather.10.cloned.1.call-update) | async-done | bytes 4194320 | tf_op jit(solution)/shard_map/all_gather | solution.py:62
  58.6 6.3 copy.24
  64.9 151.7 %all-gather.8.cloned.1.call-done = bf16[2,512,8192]{2,1,0:T(8,128)(2,1)} async-done(((bf16[2,512,2048]{2,1,0:T(8,128)(2,1)}), bf16[2,512,8192]{2,1,0:T(8,128)(2,1)}) %all-gather.8.cloned.1.call-update) | async-done | bytes 16777232 | tf_op jit(solution)/shard_map/all_gather | solution.py:50
  216.5 7.5 fusion.21
  224.0 9.0 %fusion.29 = f32[2,512,2,128]{1,3,2,0:T(8,128)S(1)} fusion(bf16[2,128,8192,1]{2,1,0,3:T(8,128)(2,1)S(1)} %bitcast.69, bf16[2,512,8192]{2,1,0:T(8,128)(2,1)} %all-gather.8.cloned.1.call-done, f32[8192]{0:T(1024)S(1)} %copy-done.2, f32[2,512]{1,0:T(2,128)S(1)} %add_rsqrt_fusion), kind=kOutput, calls=%fused_computation.49 | convolution fusion | flops 4328521728 | bytes 22056960 | tf_op jit(solution)/shard_map/dot_general | solution.py:66
  233.3 0.9 pad_maximum_fusion
  234.2 30.9 %all-gather.16.cloned.1.call-done = bf16[8192,256]{1,0:T(8,128)(2,1)} async-done(((bf16[1024,256]{1,0:T(8,128)(2,1)}), bf16[8192,256]{1,0:T(8,128)(2,1)}) %all-gather.16.cloned.1.call-update) | async-done | bytes 4194320 | tf_op jit(solution)/shard_map/all_gather | solution.py:63
  265.1 6.3 copy.28
  271.4 12.7 %convolution_convert_fusion.1 = bf16[2,512,2,128]{3,1,2,0:T(8,128)(2,1)} fusion(bf16[2,128,8192,1]{2,1,0,3:T(8,128)(2,1)} %bitcast.70, bf16[2,512,8192]{2,1,0:T(8,128)(2,1)} %all-gather.8.cloned.1.call-done, f32[8192]{0:T(1024)S(1)} %copy-done.2, f32[2,512]{1,0:T(2,128)S(1)} %add_rsqrt_fusion), kind=kOutput, calls=%fused_computation.47 | convolution fusion | flops 4328783872 | bytes 21532672 | tf_op jit(solution)/shard_map/dot_general | solution.py:66
  285.2 131.2 %all-gather.14.cloned.1.call-done = bf16[8192,1024]{1,0:T(8,128)(2,1)} async-done(((bf16[1024,1024]{1,0:T(8,128)(2,1)}), bf16[8192,1024]{1,0:T(8,128)(2,1)}) %all-gather.14.cloned.1.call-update) | async-done | bytes 16777232 | tf_op jit(solution)/shard_map/all_gather | solution.py:61
  416.4 21.4 %copy.25 = bf16[1024,8192]{1,0:T(8,128)(2,1)} copy(bf16[1024,8192]{0,1:T(8,128)(2,1)} %bitcast.63) | data formatting | bytes 33554432 | tf_op jit(solution)/shard_map/dot_general | solution.py:66
  437.9 22.4 %fusion.27 = f32[2,512,8,128]{1,3,2,0:T(8,128)S(1)} fusion(bf16[8,128,8192,1]{2,1,0,3:T(8,128)(2,1)} %bitcast.64, bf16[2,512,8192]{2,1,0:T(8,128)(2,1)} %all-gather.8.cloned.1.call-done, f32[8192]{0:T(1024)S(1)} %copy-done.2, f32[2,512]{1,0:T(2,128)S(1)} %add_rsqrt_fusion), kind=kOutput, calls=%fused_computation.48 | convolution fusion | flops 17213423616 | bytes 37785600 | tf_op jit(solution)/shard_map/dot_general | solution.py:66
  460.2 1.7 subtract_convert_fusion
  462.0 2.0 copy.26
  464.0 1.8 copy.27
  465.8 4.1 maximum_bitcast_fusion
  469.9 6.4 copy.29
  476.3 33.8 %all-gather.18.cloned.1.call-done = bf16[2,4096,2,128]{3,1,2,0:T(8,128)(2,1)} async-done(((bf16[2,512,2,128]{3,1,2,0:T(8,128)(2,1)}), bf16[2,4096,2,128]{3,1,2,0:T(8,128)(2,1)}) %all-gather.18.cloned.1.call-update) | async-done | bytes 4194320 | tf_op jit(solution)/shard_map/all_gather | solution.py:81
  510.1 2.5 broadcast_in_dim.135
  512.6 156.1 %while.19 = (s32[]{:T(128)}, f32[2,2,4,512]{3,2,1,0:T(4,128)S(1)}, f32[2,2,4,512]{3,2,1,0:T(4,128)S(1)}, f32[2,2,4,512,128]{4,3,2,1,0:T(8,128)}, s32[2,16]{1,0:T...) while((s32[]{:T(128)}, f32[2,2,4,512]{3,2,1,0:T(4,128)S(1)}, ...), condition=%wide.region_11.12_spmd, body=%wide.region_3.11_spmd.sunk | while | flops 2204700672 | bytes 64532936 | solution.py:117
  512.9 0.7 compare_reduce_fusion.2
  514.2 17.9 %conditional.2 = (f32[2,2,4,512]{3,2,1,0:T(4,128)S(1)}, f32[2,2,4,512]{3,2,1,0:T(4,128)S(1)}, f32[2,2,4,512,128]{4,3,2,1,0:T(8,128)}) conditional(s32[]{:T(128)} %convert_element_type.85, (s32[2,512]{1,0:T(2,128)S(1)}, s32[2,512]{1,0:T(2,128)S(1)}, s32[]{:T(128)}, bf16[2,4096,2,128]{3,1,2,0:T(8,128)(2,1)}, bf16[2,2,4,512,128]{4,3,2,1,0:T(8,128)(2,1)}, ...), branch_computations={%region_7.9_spmd, %region_10.10_spmd} | conditional | flops 2204647424 | bytes 64430148 | solution.py:113
  514.6 4.7 fusion
  519.3 4.1 fusion.2
  523.5 8.7 %multiply_add_fusion = f32[2,2,4,512,128]{4,3,2,1,0:T(8,128)} fusion(f32[2,2,4,512,128]{4,3,2,1,0:T(8,128)} %get-tuple-element.360, f32[2,2,4,512]{3,2,1,0:T(4,128)S(1)} %bitcast.76, f32[2,2,512,4,512]{4,2,3,1,0:T(8,128)S(1)} %get-tuple-element.437, f32[2,2,4,512]{3,2,1,0:T(4,128)S(1)} %max.5, pred[2,512,512]{1,2,0:T(8,128)(4,1)S(1)} %broadcast_compare_fusion, ...), kind=kOutput, calls=%fused_computation.7 | convolution fusion | flops 1096810496 | bytes 26279940 | tf_op jit(solution)/shard_map/while/body/eval_jaxpr/cond/branch_0_fun/shgqk,skhd->shgqd/dot_general | solution.py:105
  532.4 0.7 compare_reduce_fusion.2
  533.8 17.9 %conditional.2 = (f32[2,2,4,512]{3,2,1,0:T(4,128)S(1)}, f32[2,2,4,512]{3,2,1,0:T(4,128)S(1)}, f32[2,2,4,512,128]{4,3,2,1,0:T(8,128)}) conditional(s32[]{:T(128)} %convert_element_type.85, (s32[2,512]{1,0:T(2,128)S(1)}, s32[2,512]{1,0:T(2,128)S(1)}, s32[]{:T(128)}, bf16[2,4096,2,128]{3,1,2,0:T(8,128)(2,1)}, bf16[2,2,4,512,128]{4,3,2,1,0:T(8,128)(2,1)}, ...), branch_computations={%region_7.9_spmd, %region_10.10_spmd} | conditional | flops 2204647424 | bytes 64430148 | solution.py:113
  534.2 4.7 fusion
  538.9 4.1 fusion.2
  543.0 8.7 %multiply_add_fusion = f32[2,2,4,512,128]{4,3,2,1,0:T(8,128)} fusion(f32[2,2,4,512,128]{4,3,2,1,0:T(8,128)} %get-tuple-element.360, f32[2,2,4,512]{3,2,1,0:T(4,128)S(1)} %bitcast.76, f32[2,2,512,4,512]{4,2,3,1,0:T(8,128)S(1)} %get-tuple-element.437, f32[2,2,4,512]{3,2,1,0:T(4,128)S(1)} %max.5, pred[2,512,512]{1,2,0:T(8,128)(4,1)S(1)} %broadcast_compare_fusion, ...), kind=kOutput, calls=%fused_computation.7 | convolution fusion | flops 1096810496 | bytes 26279940 | tf_op jit(solution)/shard_map/while/body/eval_jaxpr/cond/branch_0_fun/shgqk,skhd->shgqd/dot_general | solution.py:105
  553.3 17.9 %conditional.2 = (f32[2,2,4,512]{3,2,1,0:T(4,128)S(1)}, f32[2,2,4,512]{3,2,1,0:T(4,128)S(1)}, f32[2,2,4,512,128]{4,3,2,1,0:T(8,128)}) conditional(s32[]{:T(128)} %convert_element_type.85, (s32[2,512]{1,0:T(2,128)S(1)}, s32[2,512]{1,0:T(2,128)S(1)}, s32[]{:T(128)}, bf16[2,4096,2,128]{3,1,2,0:T(8,128)(2,1)}, bf16[2,2,4,512,128]{4,3,2,1,0:T(8,128)(2,1)}, ...), branch_computations={%region_7.9_spmd, %region_10.10_spmd} | conditional | flops 2204647424 | bytes 64430148 | solution.py:113
  553.7 4.7 fusion
  558.4 4.1 fusion.2
  562.5 8.7 %multiply_add_fusion = f32[2,2,4,512,128]{4,3,2,1,0:T(8,128)} fusion(f32[2,2,4,512,128]{4,3,2,1,0:T(8,128)} %get-tuple-element.360, f32[2,2,4,512]{3,2,1,0:T(4,128)S(1)} %bitcast.76, f32[2,2,512,4,512]{4,2,3,1,0:T(8,128)S(1)} %get-tuple-element.437, f32[2,2,4,512]{3,2,1,0:T(4,128)S(1)} %max.5, pred[2,512,512]{1,2,0:T(8,128)(4,1)S(1)} %broadcast_compare_fusion, ...), kind=kOutput, calls=%fused_computation.7 | convolution fusion | flops 1096810496 | bytes 26279940 | tf_op jit(solution)/shard_map/while/body/eval_jaxpr/cond/branch_0_fun/shgqk,skhd->shgqd/dot_general | solution.py:105
  571.4 0.7 compare_reduce_fusion.2
  572.8 17.9 %conditional.2 = (f32[2,2,4,512]{3,2,1,0:T(4,128)S(1)}, f32[2,2,4,512]{3,2,1,0:T(4,128)S(1)}, f32[2,2,4,512,128]{4,3,2,1,0:T(8,128)}) conditional(s32[]{:T(128)} %convert_element_type.85, (s32[2,512]{1,0:T(2,128)S(1)}, s32[2,512]{1,0:T(2,128)S(1)}, s32[]{:T(128)}, bf16[2,4096,2,128]{3,1,2,0:T(8,128)(2,1)}, bf16[2,2,4,512,128]{4,3,2,1,0:T(8,128)(2,1)}, ...), branch_computations={%region_7.9_spmd, %region_10.10_spmd} | conditional | flops 2204647424 | bytes 64430148 | solution.py:113
  573.2 4.7 fusion
  577.9 4.1 fusion.2
  582.0 8.7 %multiply_add_fusion = f32[2,2,4,512,128]{4,3,2,1,0:T(8,128)} fusion(f32[2,2,4,512,128]{4,3,2,1,0:T(8,128)} %get-tuple-element.360, f32[2,2,4,512]{3,2,1,0:T(4,128)S(1)} %bitcast.76, f32[2,2,512,4,512]{4,2,3,1,0:T(8,128)S(1)} %get-tuple-element.437, f32[2,2,4,512]{3,2,1,0:T(4,128)S(1)} %max.5, pred[2,512,512]{1,2,0:T(8,128)(4,1)S(1)} %broadcast_compare_fusion, ...), kind=kOutput, calls=%fused_computation.7 | convolution fusion | flops 1096810496 | bytes 26279940 | tf_op jit(solution)/shard_map/while/body/eval_jaxpr/cond/branch_0_fun/shgqk,skhd->shgqd/dot_general | solution.py:105
  592.3 17.9 %conditional.2 = (f32[2,2,4,512]{3,2,1,0:T(4,128)S(1)}, f32[2,2,4,512]{3,2,1,0:T(4,128)S(1)}, f32[2,2,4,512,128]{4,3,2,1,0:T(8,128)}) conditional(s32[]{:T(128)} %convert_element_type.85, (s32[2,512]{1,0:T(2,128)S(1)}, s32[2,512]{1,0:T(2,128)S(1)}, s32[]{:T(128)}, bf16[2,4096,2,128]{3,1,2,0:T(8,128)(2,1)}, bf16[2,2,4,512,128]{4,3,2,1,0:T(8,128)(2,1)}, ...), branch_computations={%region_7.9_spmd, %region_10.10_spmd} | conditional | flops 2204647424 | bytes 64430148 | solution.py:113
  592.7 4.8 fusion
  597.5 4.1 fusion.2
  601.7 8.6 multiply_add_fusion
  610.5 0.7 compare_reduce_fusion.2
  611.9 17.8 %conditional.2 = (f32[2,2,4,512]{3,2,1,0:T(4,128)S(1)}, f32[2,2,4,512]{3,2,1,0:T(4,128)S(1)}, f32[2,2,4,512,128]{4,3,2,1,0:T(8,128)}) conditional(s32[]{:T(128)} %convert_element_type.85, (s32[2,512]{1,0:T(2,128)S(1)}, s32[2,512]{1,0:T(2,128)S(1)}, s32[]{:T(128)}, bf16[2,4096,2,128]{3,1,2,0:T(8,128)(2,1)}, bf16[2,2,4,512,128]{4,3,2,1,0:T(8,128)(2,1)}, ...), branch_computations={%region_7.9_spmd, %region_10.10_spmd} | conditional | flops 2204647424 | bytes 64430148 | solution.py:113
  612.3 4.7 fusion
  617.0 4.1 fusion.2
  621.1 8.6 multiply_add_fusion
  631.4 17.8 %conditional.2 = (f32[2,2,4,512]{3,2,1,0:T(4,128)S(1)}, f32[2,2,4,512]{3,2,1,0:T(4,128)S(1)}, f32[2,2,4,512,128]{4,3,2,1,0:T(8,128)}) conditional(s32[]{:T(128)} %convert_element_type.85, (s32[2,512]{1,0:T(2,128)S(1)}, s32[2,512]{1,0:T(2,128)S(1)}, s32[]{:T(128)}, bf16[2,4096,2,128]{3,1,2,0:T(8,128)(2,1)}, bf16[2,2,4,512,128]{4,3,2,1,0:T(8,128)(2,1)}, ...), branch_computations={%region_7.9_spmd, %region_10.10_spmd} | conditional | flops 2204647424 | bytes 64430148 | solution.py:113
  631.7 4.7 fusion
  636.5 4.1 fusion.2
  640.6 8.6 multiply_add_fusion
  649.4 0.7 compare_reduce_fusion.2
  650.8 17.9 %conditional.2 = (f32[2,2,4,512]{3,2,1,0:T(4,128)S(1)}, f32[2,2,4,512]{3,2,1,0:T(4,128)S(1)}, f32[2,2,4,512,128]{4,3,2,1,0:T(8,128)}) conditional(s32[]{:T(128)} %convert_element_type.85, (s32[2,512]{1,0:T(2,128)S(1)}, s32[2,512]{1,0:T(2,128)S(1)}, s32[]{:T(128)}, bf16[2,4096,2,128]{3,1,2,0:T(8,128)(2,1)}, bf16[2,2,4,512,128]{4,3,2,1,0:T(8,128)(2,1)}, ...), branch_computations={%region_7.9_spmd, %region_10.10_spmd} | conditional | flops 2204647424 | bytes 64430148 | solution.py:113
  651.2 4.7 fusion
  655.9 4.1 fusion.2
  660.0 8.7 %multiply_add_fusion = f32[2,2,4,512,128]{4,3,2,1,0:T(8,128)} fusion(f32[2,2,4,512,128]{4,3,2,1,0:T(8,128)} %get-tuple-element.360, f32[2,2,4,512]{3,2,1,0:T(4,128)S(1)} %bitcast.76, f32[2,2,512,4,512]{4,2,3,1,0:T(8,128)S(1)} %get-tuple-element.437, f32[2,2,4,512]{3,2,1,0:T(4,128)S(1)} %max.5, pred[2,512,512]{1,2,0:T(8,128)(4,1)S(1)} %broadcast_compare_fusion, ...), kind=kOutput, calls=%fused_computation.7 | convolution fusion | flops 1096810496 | bytes 26279940 | tf_op jit(solution)/shard_map/while/body/eval_jaxpr/cond/branch_0_fun/shgqk,skhd->shgqd/dot_general | solution.py:105
  668.7 3.1 fusion.25
  671.8 1.6 copy.30
  673.4 2.7 reshape.213
  676.1 26.4 %convolution_convert_fusion = bf16[1024,8192]{1,0:T(8,128)(2,1)} fusion(bf16[1024,1024]{1,0:T(8,128)(2,1)} %reshape.213, bf16[1024,8192]{1,0:T(8,128)(2,1)} %all-gather.20.cloned.1.call-done), kind=kOutput, calls=%fused_computation.41 | convolution fusion | flops 17188257792 | bytes 35651584 | tf_op jit(solution)/shard_map/dot_general | solution.py:120
  702.6 152.7 %reduce-scatter.2.cloned.1.call-done = bf16[1024,2048]{1,0:T(8,128)(2,1)} async-done(((bf16[1024,8192]{1,0:T(8,128)(2,1)}), bf16[1024,2048]{1,0:T(8,128)(2,1)}) %reduce-scatter.2.cloned.1.call-update) | async-done | bytes 4194320 | tf_op jit(solution)/shard_map/reduce_scatter | solution.py:125
  (100 shorter events, 10.8 us)
Async XLA Ops:
  6.5 2.9 copy-start.1
  6.5 52.0 %all-gather.10.cloned.1.call-start = ((), (), s32[]{:S(2)}) async-start(), calls=%async_computation.2 | async-start | bytes 4718592 | tf_op jit(solution)/shard_map/all_gather | solution.py:62
  7.3 209.3 %all-gather.8.cloned.1.call-start = ((), (), s32[]{:S(2)}) async-start(), calls=%async_computation.1 | async-start | bytes 20971520 | tf_op jit(solution)/shard_map/all_gather | solution.py:50
  8.0 257.0 %all-gather.16.cloned.1.call-start = ((), (), s32[]{:S(2)}) async-start(), calls=%async_computation.5 | async-start | bytes 4718592 | tf_op jit(solution)/shard_map/all_gather | solution.py:63
  8.7 407.7 %all-gather.14.cloned.1.call-start = ((), (), s32[]{:S(2)}) async-start(), calls=%async_computation.4 | async-start | bytes 18874368 | tf_op jit(solution)/shard_map/all_gather | solution.py:61
  9.3 460.5 %all-gather.12.cloned.1.call-start = ((), (), s32[]{:S(2)}) async-start(), calls=%async_computation.3 | async-start | bytes 4718592 | tf_op jit(solution)/shard_map/all_gather | solution.py:80
  64.9 159.1 %copy-start.2 = (f32[8192]{0:T(1024)S(1)}, f32[8192]{0:T(1024)}, u32[]{:S(2)}) copy-start(f32[8192]{0:T(1024)} %param.12) | copy-start | bytes 98308
  216.5 7.5 copy-start
  234.1 276.0 %all-gather.18.cloned.1.call-start = ((), (), s32[]{:S(2)}) async-start(), calls=%async_computation.6 | async-start | bytes 4718592 | tf_op jit(solution)/shard_map/all_gather | solution.py:81
  284.1 392.1 %all-gather.20.cloned.1.call-start = ((), (), s32[]{:S(2)}) async-start(), calls=%async_computation.7 | async-start | bytes 18874368 | tf_op jit(solution)/shard_map/all_gather | solution.py:122
  284.8 570.4 %reduce-scatter.2.cloned.1.call-start = ((), (), s32[]{:S(2)}) async-start(), calls=%async_computation.8 | async-start | bytes 20971520 | tf_op jit(solution)/shard_map/reduce_scatter | solution.py:125
Sparse Core Ops, SparseCore 0:
  8.9 49.5 all-gather.9
  60.4 156.0 all-gather.7
  218.1 46.8 all-gather.15
  266.5 149.8 all-gather.13
  417.9 45.0 all-gather.11
  464.4 45.6 all-gather.17
  511.7 149.8 all-gather.19
  702.7 152.5 reduce-scatter.1
where the time goes:
time: 864 us; the launch traced here: 862 us
  waiting for transfers between devices  552 us (64%)
  matrix products  177 us (20%)
  other arithmetic  62 us (7%)
  local copies, waits for them, and re-layouts  51.1 us (6%)
  between operations  13.6 us (2%)
    reduce_scatter x1, waiting for transfers between devices, per_device(): lax.psum_scatter(terms.astype(jnp.bfloat16), 'tp', scatter_dimension=1, t...  153 us
    all_gather x1, waiting for transfers between devices, per_device(): whole = lax.all_gather(tokens, 'tp', axis=2, tiled=True)  152 us
    all_gather x1, waiting for transfers between devices, per_device(): lax.all_gather(w_query, 'ctx', axis=0, tiled=True)  131 us
    dot_general x8, matrix products, update(): jnp.einsum('shgqk,skhd->shgqd', weights.astype(jnp.bfloat16), value_block...  69.1 us
    all_gather x1, waiting for transfers between devices, per_device(): lax.all_gather(w_key, 'ctx', axis=0, tiled=True)  48 us
    dot_general x3, matrix products, per_device(): jnp.dot(normed, piece, preferred_element_type=jnp.float32)  44.1 us
    dot_general x8, matrix products, update(): jnp.einsum('shgqd,skhd->shgqk', query, key_block, preferred_element_type=...  37.6 us
    dot_general x3, local copies, waits for them, and re-layouts, per_device(): jnp.dot(normed, piece, preferred_element_type=jnp.float32)  34.1 us
  transfers between devices with their start and end apart: 8, of which 6 were waited for; matrix products, arithmetic and copies ran while one was open for 31% of the time, Pallas kernels for 0%

commit v1 on v0

--- a/solution.py
+++ b/solution.py
@@ -47,7 +47,9 @@
     total_rows = sequence_batch * rows_dev
     factor = 1.0 / math.sqrt(head_size)
     rank = lax.axis_index("ctx")
-    whole = lax.all_gather(tokens, "tp", axis=2, tiled=True)
+    whole = jnp.concatenate(
+        lax.all_to_all(jnp.stack([tokens for _ in range(lax.axis_size("tp"))]), "tp", 0, 0), axis=2
+    )
     normed = normalize(whole.reshape(total_rows, whole.shape[2]), norm_gain)
     query_pos = positions_of(span_order, rank * rows_dev, rows_dev, block_rows)
     latest = jnp.max(query_pos, axis=1)

time: 864 us -> 856 us (level)
  waiting for transfers between devices: 552 us -> 503 us
  local copies, waits for them, and re-layouts: 51.1 us -> 80.6 us
    all_gather x1 -> x0, waiting for transfers between devices: 152 us -> none  [per_device(): whole = lax.all_gather(tokens, 'tp', axis=2, tiled=True)]
    all_to_all x0 -> x1, waiting for transfers between devices: none -> 125 us  [per_device(): lax.all_to_all(jnp.stack([tokens for _ in range(lax.axis_size('tp'))]), '...]
    all_gather x1, waiting for transfers between devices: 33.8 us -> 0.01 us  [per_device(): value_piece = lax.all_gather(own_values, 'ctx', axis=1, tiled=True)]
    all_gather x1, waiting for transfers between devices: 30.9 us -> 0.02 us  [per_device(): lax.all_gather(value_weight, 'ctx', axis=0, tiled=True)]
    all_gather x1, waiting for transfers between devices: 0.01 us -> 28.9 us  [per_device(): key_piece = lax.all_gather(turned, 'ctx', axis=1, tiled=True)]
    all_to_all x0 -> x1, local copies, waits for them, and re-layouts: none -> 21.7 us  [per_device(): lax.all_to_all(jnp.stack([tokens for _ in range(lax.axis_size('tp'))]), '...]
    all_gather x1, waiting for transfers between devices: 131 us -> 145 us  [per_device(): lax.all_gather(w_query, 'ctx', axis=0, tiled=True)]
  transfers between devices with their start and end apart: 8 -> 8, of which waited for: 6 -> 5; matrix products, arithmetic and copies ran while one was open for 31% -> 34% of each run, Pallas kernels for 0% -> 0%
where the time goes in v1:
time: 856 us; the launch traced here: 853 us
  waiting for transfers between devices  503 us (59%)
  matrix products  172 us (20%)
  local copies, waits for them, and re-layouts  80.6 us (9%)
  other arithmetic  70.1 us (8%)
  between operations  13.7 us (2%)
    reduce_scatter x1, waiting for transfers between devices, per_device(): lax.psum_scatter(terms.astype(jnp.bfloat16), 'tp', scatter_dimension=1, t...  152 us
    all_gather x1, waiting for transfers between devices, per_device(): lax.all_gather(w_query, 'ctx', axis=0, tiled=True)  145 us
    all_to_all x1, waiting for transfers between devices, per_device(): lax.all_to_all(jnp.stack([tokens for _ in range(lax.axis_size('tp'))]), '...  125 us
    dot_general x8, matrix products, update(): jnp.einsum('shgqk,skhd->shgqd', weights.astype(jnp.bfloat16), value_block...  68.9 us
    all_gather x1, waiting for transfers between devices, per_device(): lax.all_gather(w_key, 'ctx', axis=0, tiled=True)  49.7 us
    dot_general x3, matrix products, per_device(): jnp.dot(normed, piece, preferred_element_type=jnp.float32)  38.8 us
    dot_general x8, matrix products, update(): jnp.einsum('shgqd,skhd->shgqk', query, key_block, preferred_element_type=...  38.1 us
    dot_general x3, local copies, waits for them, and re-layouts, per_device(): jnp.dot(normed, piece, preferred_element_type=jnp.float32)  34.1 us
  transfers between devices with their start and end apart: 8, of which 5 were waited for; matrix products, arithmetic and copies ran while one was open for 34% of the time, Pallas kernels for 0%

profile of v1, /device:TPU:0, one launch (start us, length us, event | category | flops | bytes accessed | tf_op | source)
XLA Modules:
  0.0 853.0 jit_solution(5562048849731492615)
XLA Ops:
  6.5 7.4 stack.2
  14.0 7.1 all-to-all-start
  22.9 1.0 multiply_cosine_fusion
  23.9 49.7 %all-gather.7.cloned.1.call-done = bf16[8192,256]{1,0:T(8,128)(2,1)} async-done(((bf16[1024,256]{1,0:T(8,128)(2,1)}), bf16[8192,256]{1,0:T(8,128)(2,1)}) %all-gather.7.cloned.1.call-update) | async-done | bytes 4194320 | tf_op jit(solution)/shard_map/all_gather | solution.py:64
  73.6 6.3 copy.45
  79.9 125.0 %all-to-all-done = bf16[4,2,512,2048]{3,2,1,0:T(8,128)(2,1)} async-done(((bf16[4,2,512,2048]{3,2,1,0:T(8,128)(2,1)}), bf16[4,2,512,2048]{3,2,1,0:T(8,128)(2,1)}, u32[]{:S(2)}, u32[]{:S(2)}) %all-to-all-start) | async-done | bytes 16777248 | tf_op jit(solution)/shard_map/all_to_all | solution.py:51
  204.9 21.7 %copy.44 = bf16[4,2,512,2048]{2,3,0,1:T(8,128)(2,1)} copy(bf16[4,2,512,2048]{3,2,1,0:T(8,128)(2,1)} %all-to-all-done) | data formatting | bytes 33554432 | tf_op jit(solution)/shard_map/all_to_all | solution.py:51
  226.5 10.5 %fusion.21 = f32[2,512]{1,0:T(2,128)S(1)} fusion(bf16[4,2,512,2048]{2,3,0,1:T(8,128)(2,1)} %copy.44), kind=kLoop, calls=%fused_computation.37 | loop fusion | flops 25164800 | bytes 16781312 | tf_op jit(solution)/shard_map/reduce_sum | solution.py:15
  237.5 4.1 fusion.23
  241.6 6.5 fusion.30
  248.1 1.4 subtract_convert_fusion.1
  249.5 0.8 pad_maximum_fusion
  251.0 6.3 copy.51
  257.3 10.7 %convolution_convert_fusion.1 = bf16[2,512,2,128]{3,1,2,0:T(8,128)(2,1)} fusion(bf16[2,512,8192,1]{1,2,3,0:T(8,128)(2,1)} %bitcast.69, bf16[2,128,8192,1]{2,1,0,3:T(8,128)(2,1)} %bitcast.78), kind=kOutput, calls=%fused_computation.46 | convolution fusion | flops 4295229440 | bytes 21495808 | tf_op jit(solution)/shard_map/dot_general | solution.py:68
  269.0 28.9 %all-gather.9.cloned.1.call-done = bf16[2,4096,2,128]{1,3,2,0:T(8,128)(2,1)} async-done(((bf16[2,512,2,128]{1,3,2,0:T(8,128)(2,1)}), bf16[2,4096,2,128]{1,3,2,0:T(8,128)(2,1)}) %all-gather.9.cloned.1.call-update) | async-done | bytes 4194320 | tf_op jit(solution)/shard_map/all_gather | solution.py:82
  297.9 6.4 copy.53
  304.2 145.0 %all-gather.11.cloned.1.call-done = bf16[8192,1024]{1,0:T(8,128)(2,1)} async-done(((bf16[1024,1024]{1,0:T(8,128)(2,1)}), bf16[8192,1024]{1,0:T(8,128)(2,1)}) %all-gather.11.cloned.1.call-update) | async-done | bytes 16777232 | tf_op jit(solution)/shard_map/all_gather | solution.py:63
  449.3 21.5 %copy.47 = bf16[1024,8192]{1,0:T(8,128)(2,1)} copy(bf16[1024,8192]{0,1:T(8,128)(2,1)} %bitcast.71) | data formatting | bytes 33554432 | tf_op jit(solution)/shard_map/dot_general | solution.py:68
  470.7 21.7 %fusion.31 = f32[2,512,8,128]{1,3,2,0:T(8,128)S(1)} fusion(bf16[2,512,8192,1]{1,2,3,0:T(8,128)(2,1)} %bitcast.70, bf16[8,128,8192,1]{2,1,0,3:T(8,128)(2,1)} %bitcast.72), kind=kOutput, calls=%fused_computation.70 | convolution fusion | flops 17179869184 | bytes 37748736 | tf_op jit(solution)/shard_map/dot_general | solution.py:68
  492.4 1.7 subtract_convert_fusion
  494.1 2.0 copy.49
  496.1 1.8 copy.50
  497.9 4.1 maximum_bitcast_fusion
  502.0 2.5 broadcast_in_dim.135
  504.5 156.3 %while.19 = (s32[]{:T(128)}, f32[2,2,4,512]{3,2,1,0:T(4,128)S(1)}, f32[2,2,4,512]{3,2,1,0:T(4,128)S(1)}, f32[2,2,4,512,128]{4,3,2,1,0:T(8,128)}, s32[2,16]{1,0:T...) while((s32[]{:T(128)}, f32[2,2,4,512]{3,2,1,0:T(4,128)S(1)}, ...), condition=%wide.region_11.12_spmd, body=%wide.region_3.11_spmd.sunk | while | flops 2204700672 | bytes 64532936 | solution.py:119
  504.9 0.7 compare_reduce_fusion.2
  506.3 18.3 %conditional.2 = (f32[2,2,4,512]{3,2,1,0:T(4,128)S(1)}, f32[2,2,4,512]{3,2,1,0:T(4,128)S(1)}, f32[2,2,4,512,128]{4,3,2,1,0:T(8,128)}) conditional(s32[]{:T(128)} %convert_element_type.101, (s32[2,512]{1,0:T(2,128)S(1)}, s32[2,512]{1,0:T(2,128)S(1)}, s32[]{:T(128)}, bf16[2,4096,2,128]{3,1,2,0:T(8,128)(2,1)}, bf16[2,2,4,512,128]{4,3,2,1,0:T(8,128)(2,1)}, ...), branch_computations={%region_7.9_spmd, %region_10.10_spmd} | conditional | flops 2204647424 | bytes 64430148 | solution.py:115
  506.7 5.1 fusion
  511.8 4.1 fusion.2
  516.0 8.6 %multiply_add_fusion = f32[2,2,4,512,128]{4,3,2,1,0:T(8,128)} fusion(f32[2,2,4,512,128]{4,3,2,1,0:T(8,128)} %get-tuple-element.360, f32[2,2,4,512]{3,2,1,0:T(4,128)S(1)} %bitcast.84, f32[2,2,512,4,512]{4,2,3,1,0:T(8,128)S(1)} %get-tuple-element.457, f32[2,2,4,512]{3,2,1,0:T(4,128)S(1)} %max.5, pred[2,512,512]{1,2,0:T(8,128)(4,1)S(1)} %broadcast_compare_fusion, ...), kind=kOutput, calls=%fused_computation.7 | convolution fusion | flops 1096810496 | bytes 26279940 | tf_op jit(solution)/shard_map/while/body/eval_jaxpr/cond/branch_0_fun/shgqk,skhd->shgqd/dot_general | solution.py:107
  524.8 0.7 compare_reduce_fusion.2
  526.2 17.9 %conditional.2 = (f32[2,2,4,512]{3,2,1,0:T(4,128)S(1)}, f32[2,2,4,512]{3,2,1,0:T(4,128)S(1)}, f32[2,2,4,512,128]{4,3,2,1,0:T(8,128)}) conditional(s32[]{:T(128)} %convert_element_type.101, (s32[2,512]{1,0:T(2,128)S(1)}, s32[2,512]{1,0:T(2,128)S(1)}, s32[]{:T(128)}, bf16[2,4096,2,128]{3,1,2,0:T(8,128)(2,1)}, bf16[2,2,4,512,128]{4,3,2,1,0:T(8,128)(2,1)}, ...), branch_computations={%region_7.9_spmd, %region_10.10_spmd} | conditional | flops 2204647424 | bytes 64430148 | solution.py:115
  526.6 4.7 fusion
  531.3 4.1 fusion.2
  535.4 8.6 %multiply_add_fusion = f32[2,2,4,512,128]{4,3,2,1,0:T(8,128)} fusion(f32[2,2,4,512,128]{4,3,2,1,0:T(8,128)} %get-tuple-element.360, f32[2,2,4,512]{3,2,1,0:T(4,128)S(1)} %bitcast.84, f32[2,2,512,4,512]{4,2,3,1,0:T(8,128)S(1)} %get-tuple-element.457, f32[2,2,4,512]{3,2,1,0:T(4,128)S(1)} %max.5, pred[2,512,512]{1,2,0:T(8,128)(4,1)S(1)} %broadcast_compare_fusion, ...), kind=kOutput, calls=%fused_computation.7 | convolution fusion | flops 1096810496 | bytes 26279940 | tf_op jit(solution)/shard_map/while/body/eval_jaxpr/cond/branch_0_fun/shgqk,skhd->shgqd/dot_general | solution.py:107
  545.6 17.9 %conditional.2 = (f32[2,2,4,512]{3,2,1,0:T(4,128)S(1)}, f32[2,2,4,512]{3,2,1,0:T(4,128)S(1)}, f32[2,2,4,512,128]{4,3,2,1,0:T(8,128)}) conditional(s32[]{:T(128)} %convert_element_type.101, (s32[2,512]{1,0:T(2,128)S(1)}, s32[2,512]{1,0:T(2,128)S(1)}, s32[]{:T(128)}, bf16[2,4096,2,128]{3,1,2,0:T(8,128)(2,1)}, bf16[2,2,4,512,128]{4,3,2,1,0:T(8,128)(2,1)}, ...), branch_computations={%region_7.9_spmd, %region_10.10_spmd} | conditional | flops 2204647424 | bytes 64430148 | solution.py:115
  546.0 4.7 fusion
  550.7 4.1 fusion.2
  554.9 8.6 %multiply_add_fusion = f32[2,2,4,512,128]{4,3,2,1,0:T(8,128)} fusion(f32[2,2,4,512,128]{4,3,2,1,0:T(8,128)} %get-tuple-element.360, f32[2,2,4,512]{3,2,1,0:T(4,128)S(1)} %bitcast.84, f32[2,2,512,4,512]{4,2,3,1,0:T(8,128)S(1)} %get-tuple-element.457, f32[2,2,4,512]{3,2,1,0:T(4,128)S(1)} %max.5, pred[2,512,512]{1,2,0:T(8,128)(4,1)S(1)} %broadcast_compare_fusion, ...), kind=kOutput, calls=%fused_computation.7 | convolution fusion | flops 1096810496 | bytes 26279940 | tf_op jit(solution)/shard_map/while/body/eval_jaxpr/cond/branch_0_fun/shgqk,skhd->shgqd/dot_general | solution.py:107
  565.1 17.8 %conditional.2 = (f32[2,2,4,512]{3,2,1,0:T(4,128)S(1)}, f32[2,2,4,512]{3,2,1,0:T(4,128)S(1)}, f32[2,2,4,512,128]{4,3,2,1,0:T(8,128)}) conditional(s32[]{:T(128)} %convert_element_type.101, (s32[2,512]{1,0:T(2,128)S(1)}, s32[2,512]{1,0:T(2,128)S(1)}, s32[]{:T(128)}, bf16[2,4096,2,128]{3,1,2,0:T(8,128)(2,1)}, bf16[2,2,4,512,128]{4,3,2,1,0:T(8,128)(2,1)}, ...), branch_computations={%region_7.9_spmd, %region_10.10_spmd} | conditional | flops 2204647424 | bytes 64430148 | solution.py:115
  565.5 4.7 fusion
  570.2 4.1 fusion.2
  574.3 8.6 %multiply_add_fusion = f32[2,2,4,512,128]{4,3,2,1,0:T(8,128)} fusion(f32[2,2,4,512,128]{4,3,2,1,0:T(8,128)} %get-tuple-element.360, f32[2,2,4,512]{3,2,1,0:T(4,128)S(1)} %bitcast.84, f32[2,2,512,4,512]{4,2,3,1,0:T(8,128)S(1)} %get-tuple-element.457, f32[2,2,4,512]{3,2,1,0:T(4,128)S(1)} %max.5, pred[2,512,512]{1,2,0:T(8,128)(4,1)S(1)} %broadcast_compare_fusion, ...), kind=kOutput, calls=%fused_computation.7 | convolution fusion | flops 1096810496 | bytes 26279940 | tf_op jit(solution)/shard_map/while/body/eval_jaxpr/cond/branch_0_fun/shgqk,skhd->shgqd/dot_general | solution.py:107
  584.5 17.8 %conditional.2 = (f32[2,2,4,512]{3,2,1,0:T(4,128)S(1)}, f32[2,2,4,512]{3,2,1,0:T(4,128)S(1)}, f32[2,2,4,512,128]{4,3,2,1,0:T(8,128)}) conditional(s32[]{:T(128)} %convert_element_type.101, (s32[2,512]{1,0:T(2,128)S(1)}, s32[2,512]{1,0:T(2,128)S(1)}, s32[]{:T(128)}, bf16[2,4096,2,128]{3,1,2,0:T(8,128)(2,1)}, bf16[2,2,4,512,128]{4,3,2,1,0:T(8,128)(2,1)}, ...), branch_computations={%region_7.9_spmd, %region_10.10_spmd} | conditional | flops 2204647424 | bytes 64430148 | solution.py:115
  584.9 4.7 fusion
  589.6 4.1 fusion.2
  593.8 8.6 %multiply_add_fusion = f32[2,2,4,512,128]{4,3,2,1,0:T(8,128)} fusion(f32[2,2,4,512,128]{4,3,2,1,0:T(8,128)} %get-tuple-element.360, f32[2,2,4,512]{3,2,1,0:T(4,128)S(1)} %bitcast.84, f32[2,2,512,4,512]{4,2,3,1,0:T(8,128)S(1)} %get-tuple-element.457, f32[2,2,4,512]{3,2,1,0:T(4,128)S(1)} %max.5, pred[2,512,512]{1,2,0:T(8,128)(4,1)S(1)} %broadcast_compare_fusion, ...), kind=kOutput, calls=%fused_computation.7 | convolution fusion | flops 1096810496 | bytes 26279940 | tf_op jit(solution)/shard_map/while/body/eval_jaxpr/cond/branch_0_fun/shgqk,skhd->shgqd/dot_general | solution.py:107
  604.0 17.9 %conditional.2 = (f32[2,2,4,512]{3,2,1,0:T(4,128)S(1)}, f32[2,2,4,512]{3,2,1,0:T(4,128)S(1)}, f32[2,2,4,512,128]{4,3,2,1,0:T(8,128)}) conditional(s32[]{:T(128)} %convert_element_type.101, (s32[2,512]{1,0:T(2,128)S(1)}, s32[2,512]{1,0:T(2,128)S(1)}, s32[]{:T(128)}, bf16[2,4096,2,128]{3,1,2,0:T(8,128)(2,1)}, bf16[2,2,4,512,128]{4,3,2,1,0:T(8,128)(2,1)}, ...), branch_computations={%region_7.9_spmd, %region_10.10_spmd} | conditional | flops 2204647424 | bytes 64430148 | solution.py:115
  604.3 4.8 fusion
  609.1 4.1 fusion.2
  613.2 8.6 %multiply_add_fusion = f32[2,2,4,512,128]{4,3,2,1,0:T(8,128)} fusion(f32[2,2,4,512,128]{4,3,2,1,0:T(8,128)} %get-tuple-element.360, f32[2,2,4,512]{3,2,1,0:T(4,128)S(1)} %bitcast.84, f32[2,2,512,4,512]{4,2,3,1,0:T(8,128)S(1)} %get-tuple-element.457, f32[2,2,4,512]{3,2,1,0:T(4,128)S(1)} %max.5, pred[2,512,512]{1,2,0:T(8,128)(4,1)S(1)} %broadcast_compare_fusion, ...), kind=kOutput, calls=%fused_computation.7 | convolution fusion | flops 1096810496 | bytes 26279940 | tf_op jit(solution)/shard_map/while/body/eval_jaxpr/cond/branch_0_fun/shgqk,skhd->shgqd/dot_general | solution.py:107
  623.4 17.9 %conditional.2 = (f32[2,2,4,512]{3,2,1,0:T(4,128)S(1)}, f32[2,2,4,512]{3,2,1,0:T(4,128)S(1)}, f32[2,2,4,512,128]{4,3,2,1,0:T(8,128)}) conditional(s32[]{:T(128)} %convert_element_type.101, (s32[2,512]{1,0:T(2,128)S(1)}, s32[2,512]{1,0:T(2,128)S(1)}, s32[]{:T(128)}, bf16[2,4096,2,128]{3,1,2,0:T(8,128)(2,1)}, bf16[2,2,4,512,128]{4,3,2,1,0:T(8,128)(2,1)}, ...), branch_computations={%region_7.9_spmd, %region_10.10_spmd} | conditional | flops 2204647424 | bytes 64430148 | solution.py:115
  623.8 4.7 fusion
  628.6 4.1 fusion.2
  632.7 8.6 %multiply_add_fusion = f32[2,2,4,512,128]{4,3,2,1,0:T(8,128)} fusion(f32[2,2,4,512,128]{4,3,2,1,0:T(8,128)} %get-tuple-element.360, f32[2,2,4,512]{3,2,1,0:T(4,128)S(1)} %bitcast.84, f32[2,2,512,4,512]{4,2,3,1,0:T(8,128)S(1)} %get-tuple-element.457, f32[2,2,4,512]{3,2,1,0:T(4,128)S(1)} %max.5, pred[2,512,512]{1,2,0:T(8,128)(4,1)S(1)} %broadcast_compare_fusion, ...), kind=kOutput, calls=%fused_computation.7 | convolution fusion | flops 1096810496 | bytes 26279940 | tf_op jit(solution)/shard_map/while/body/eval_jaxpr/cond/branch_0_fun/shgqk,skhd->shgqd/dot_general | solution.py:107
  642.9 17.8 %conditional.2 = (f32[2,2,4,512]{3,2,1,0:T(4,128)S(1)}, f32[2,2,4,512]{3,2,1,0:T(4,128)S(1)}, f32[2,2,4,512,128]{4,3,2,1,0:T(8,128)}) conditional(s32[]{:T(128)} %convert_element_type.101, (s32[2,512]{1,0:T(2,128)S(1)}, s32[2,512]{1,0:T(2,128)S(1)}, s32[]{:T(128)}, bf16[2,4096,2,128]{3,1,2,0:T(8,128)(2,1)}, bf16[2,2,4,512,128]{4,3,2,1,0:T(8,128)(2,1)}, ...), branch_computations={%region_7.9_spmd, %region_10.10_spmd} | conditional | flops 2204647424 | bytes 64430148 | solution.py:115
  643.3 4.7 fusion
  648.0 4.1 fusion.2
  652.1 8.6 %multiply_add_fusion = f32[2,2,4,512,128]{4,3,2,1,0:T(8,128)} fusion(f32[2,2,4,512,128]{4,3,2,1,0:T(8,128)} %get-tuple-element.360, f32[2,2,4,512]{3,2,1,0:T(4,128)S(1)} %bitcast.84, f32[2,2,512,4,512]{4,2,3,1,0:T(8,128)S(1)} %get-tuple-element.457, f32[2,2,4,512]{3,2,1,0:T(4,128)S(1)} %max.5, pred[2,512,512]{1,2,0:T(8,128)(4,1)S(1)} %broadcast_compare_fusion, ...), kind=kOutput, calls=%fused_computation.7 | convolution fusion | flops 1096810496 | bytes 26279940 | tf_op jit(solution)/shard_map/while/body/eval_jaxpr/cond/branch_0_fun/shgqk,skhd->shgqd/dot_general | solution.py:107
  660.7 2.9 fusion.24
  663.6 1.6 copy.54
  665.2 2.7 reshape.240
  667.9 26.4 %convolution_convert_fusion = bf16[1024,8192]{1,0:T(8,128)(2,1)} fusion(bf16[1024,1024]{1,0:T(8,128)(2,1)} %reshape.240, bf16[1024,8192]{1,0:T(8,128)(2,1)} %all-gather.17.cloned.1.call-done), kind=kOutput, calls=%fused_computation.40 | convolution fusion | flops 17188257792 | bytes 35651584 | tf_op jit(solution)/shard_map/dot_general | solution.py:122
  694.4 151.8 %reduce-scatter.2.cloned.1.call-done = bf16[1024,2048]{1,0:T(8,128)(2,1)} async-done(((bf16[1024,8192]{1,0:T(8,128)(2,1)}), bf16[1024,2048]{1,0:T(8,128)(2,1)}) %reduce-scatter.2.cloned.1.call-update) | async-done | bytes 4194320 | tf_op jit(solution)/shard_map/reduce_scatter | solution.py:127
  (111 shorter events, 13.0 us)
Async XLA Ops:
  14.0 8.7 %copy-start.6 = (f32[8192]{0:T(1024)S(1)}, f32[8192]{0:T(1024)}, u32[]{:S(2)}) copy-start(f32[8192]{0:T(1024)} %param.12) | copy-start | bytes 98308
  14.0 8.8 %copy-start.5 = (s32[2,16]{1,0:T(2,128)S(1)}, s32[2,16]{1,0:T(2,128)}, u32[]{:S(2)}) copy-start(s32[2,16]{1,0:T(2,128)} %param.13) | copy-start | bytes 388
  14.0 190.9 %all-to-all-start = ((bf16[4,2,512,2048]{3,2,1,0:T(8,128)(2,1)}), bf16[4,2,512,2048]{3,2,1,0:T(8,128)(2,1)}, u32[]{:S(2)}, u32[]{:S(2)}) async-start(bf16[4,2,512,2048]{3,2,1,0:T(8,128)(2,1)} %stack.2), calls=%async_computation | async-start | bytes 33554432 | tf_op jit(solution)/shard_map/all_to_all | solution.py:51
  21.1 52.5 %all-gather.7.cloned.1.call-start = ((), (), s32[]{:S(2)}) async-start(), calls=%async_computation.2 | async-start | bytes 4718592 | tf_op jit(solution)/shard_map/all_gather | solution.py:64
  21.9 229.1 %all-gather.13.cloned.1.call-start = ((), (), s32[]{:S(2)}) async-start(), calls=%async_computation.5 | async-start | bytes 4718592 | tf_op jit(solution)/shard_map/all_gather | solution.py:65
  22.6 275.3 %all-gather.9.cloned.1.call-start = ((), (), s32[]{:S(2)}) async-start(), calls=%async_computation.3 | async-start | bytes 4718592 | tf_op jit(solution)/shard_map/all_gather | solution.py:82
  23.9 224.2 %copy-start.3 = (f32[2,512,64]{1,2,0:T(8,128)}, f32[2,512,64]{1,2,0:T(8,128)S(1)}, u32[]{:S(2)}) copy-start(f32[2,512,64]{1,2,0:T(8,128)S(1)} %get-tuple-element.465) | copy-start | bytes 786436
  226.5 10.9 %copy-start = (bf16[4,2,512,2048]{2,3,0,1:T(8,128)(2,1)S(1)}, bf16[4,2,512,2048]{2,3,0,1:T(8,128)(2,1)}, u32[]{:S(2)}) copy-start(bf16[4,2,512,2048]{2,3,0,1:T(8,128)(2,1)} %copy.44) | copy-start | bytes 50331652
  237.5 4.2 copy-start.2
  241.6 6.5 copy-start.1
  250.4 198.9 %all-gather.11.cloned.1.call-start = ((), (), s32[]{:S(2)}) async-start(), calls=%async_computation.4 | async-start | bytes 18874368 | tf_op jit(solution)/shard_map/all_gather | solution.py:63
  250.9 251.0 %all-gather.15.cloned.1.call-start = ((), (), s32[]{:S(2)}) async-start(), calls=%async_computation.6 | async-start | bytes 4718592 | tf_op jit(solution)/shard_map/all_gather | solution.py:83
  268.0 399.9 %all-gather.17.cloned.1.call-start = ((), (), s32[]{:S(2)}) async-start(), calls=%async_computation.7 | async-start | bytes 18874368 | tf_op jit(solution)/shard_map/all_gather | solution.py:124
  268.6 577.6 %reduce-scatter.2.cloned.1.call-start = ((), (), s32[]{:S(2)}) async-start(), calls=%async_computation.8 | async-start | bytes 20971520 | tf_op jit(solution)/shard_map/reduce_scatter | solution.py:127
  470.7 21.7 %copy-start.4 = (f32[2,512,64]{1,2,0:T(8,128)S(1)}, f32[2,512,64]{1,2,0:T(8,128)}, u32[]{:S(2)}) copy-start(f32[2,512,64]{1,2,0:T(8,128)} %copy-done.3) | copy-start | bytes 786436
Sparse Core Ops, SparseCore 0:
  23.5 49.9 all-gather.6
  75.2 45.6 all-gather.12
  250.5 47.3 all-gather.8
  299.3 149.8 all-gather.10
  450.7 45.0 all-gather.14
  497.3 149.8 all-gather.16
  694.5 151.6 reduce-scatter.1
